TPU v7x, 256 devices: a whole 4x4x8 slice. The times are simulated.
256 devices in a mesh: scan: 8 (over y, core), ascan: 32 (over x, z).
Axes of the slice: x: 4, y: 4, z: 8, core: 2. Of those that a mesh axis runs over, the one named last changes fastest.
Arguments:
- spectra: bfloat16 [16, 4, 4096, 2048], P('scan', None, 'ascan'), may hold values from -8 to 8
- surface_top: int32 [16, 4096], P('scan', 'ascan'), may hold values from 0 to 3, as said below
- surface_bottom: int32 [16, 4096], P('scan', 'ascan'), may hold values from 1 to 8, as said below
Outputs:
- angiogram: float32 [16, 1024, 4096], P('scan', 'ascan')
- structure_map: float32 [16, 1024, 4096], P('scan', 'ascan')
- speckle_map: float32 [16, 1024, 4096], P('scan', 'ascan')
- mean_flow: float32 [], replicated
Inputs may be any that keep to these rules, and one draw needn't show every extreme that they name: surface_top counts tiles of 128 depth rows. surface_bottom is greater than surface_top of the same A-scan.
All inputs are finite; a program needn't handle non-finite values.
Results may differ from a plain program's by a relative error of at most 0.0032.
Values sent between devices are 32-bit elements; how exact they have to be, the bound alone decides.
A program may use at most 128 MiB of HBM per device.

v0:
```python
import math

import jax
import jax.numpy as jnp
from jax import lax
from jax.sharding import Mesh
from jax.sharding import PartitionSpec as P

REPEATS = 4
BINS = 2048
BANDS = 4
TILE = 128
BAND_BINS = 512
DEPTH = 1024
SCAN_ASCAN = ("scan_0", "scan_1", "ascan_0", "ascan_1")
ASCAN = ("ascan_0", "ascan_1")
SCAN = ("scan_0", "scan_1")


FLOOR_SHARE = 0.05
VARIANCE_SCALE = 0.1


def over_axes(value, axes):
    for axis in axes:
        value = lax.psum(value, axis)
    return value


def in_one_piece(arrays, axis, split_dim, concat_dim, along):
    both = jnp.concatenate(arrays, axis=along)
    filled, at, finished = (
        lax.all_to_all(both, axis, split_axis=split_dim, concat_axis=concat_dim, tiled=True),
        0,
        [],
    )
    for a in arrays:
        finished.append(lax.slice_in_dim(filled, at, at + a.shape[along], axis=along))
        at += a.shape[along]
    return tuple(finished)


def make_table():
    sample = jnp.arange(BAND_BINS, dtype=jnp.int32)
    depth_index = jnp.arange(DEPTH, dtype=jnp.int32)
    product = sample[:, None] * depth_index[None, :] % BINS
    phase_angle = product.astype(jnp.float32) * (2.0 * math.pi / BINS)
    window = jnp.sin(math.pi * (sample.astype(jnp.float32) + 0.5) / BAND_BINS) ** 2
    cosine = window[:, None] * jnp.cos(phase_angle)
    sine = window[:, None] * jnp.sin(phase_angle)
    return jnp.concatenate([cosine, sine], axis=1).astype(jnp.bfloat16)


def band_moments(spectra, table_part, surface_top, surface_bottom):
    scan_count, repeat_count, ascan_count, bin_count = spectra.shape
    depth_width = table_part.shape[1] // 2
    flat = spectra.reshape(scan_count * repeat_count * ascan_count, BANDS, BAND_BINS)
    similarity_total = jnp.zeros((scan_count, ascan_count, depth_width), jnp.float32)
    amplitude_total = jnp.zeros((scan_count, ascan_count, depth_width), jnp.float32)
    variance_total = jnp.zeros((scan_count, ascan_count, depth_width), jnp.float32)
    for band_index in range(BANDS):
        profile = jnp.dot(flat[:, band_index, :], table_part, preferred_element_type=jnp.float32)
        profile = profile.reshape(scan_count, repeat_count, ascan_count, 2 * depth_width)
        amplitude = jnp.sqrt(profile[..., :depth_width] ** 2 + profile[..., depth_width:] ** 2)
        earlier = amplitude[:, :-1]
        later = amplitude[:, 1:]
        similarity = (
            2.0 * earlier * later / jnp.maximum(earlier**2 + later**2, FLOOR_SHARE * BAND_BINS)
        )
        similarity_total = similarity_total + jnp.sum(similarity, axis=1)
        amplitude_total = amplitude_total + jnp.sum(amplitude, axis=1)
        repeat_mean = jnp.mean(amplitude, axis=1, keepdims=True)
        variance_total = variance_total + jnp.mean((amplitude - repeat_mean) ** 2, axis=1)
    depth_rows = jnp.arange(depth_width, dtype=jnp.int32)
    lower = depth_rows[None, None, :] >= surface_top[..., None] * TILE
    upper = depth_rows[None, None, :] < surface_bottom[..., None] * TILE
    inside = (lower & upper).astype(jnp.float32)
    decorrelation = (1.0 - similarity_total / (BANDS * (REPEATS - 1))) * inside
    structure = amplitude_total / (BANDS * REPEATS) / math.sqrt(BAND_BINS) * inside
    speckle = variance_total / BANDS / (VARIANCE_SCALE * BAND_BINS) * inside
    return (decorrelation, structure, speckle, jnp.sum(decorrelation), jnp.sum(inside))


def body(spectra, surface_top, surface_bottom):
    dft_table = make_table()
    decorrelation, structure, speckle, flow_sum, tissue_count = band_moments(
        spectra, dft_table, surface_top, surface_bottom
    )
    totals = (over_axes(flow_sum, SCAN_ASCAN), over_axes(tissue_count, SCAN_ASCAN))
    mean_flow = totals[0] / totals[1]
    decorrelation, structure, speckle = in_one_piece(
        (decorrelation, structure, speckle), ASCAN, 2, 1, 0
    )
    padded = jnp.pad(decorrelation, ((0, 0), (1, 1), (0, 0)))
    smoothed = (padded[:, :-2] + padded[:, 1:-1] + padded[:, 2:]) / 3.0
    angiogram = jnp.swapaxes(smoothed / mean_flow, 1, 2)
    return (angiogram, jnp.swapaxes(structure, 1, 2), jnp.swapaxes(speckle, 1, 2), mean_flow)


def solution(mesh):
    finer = Mesh(mesh.devices.reshape(4, 2, 4, 8), ("scan_0", "scan_1", "ascan_0", "ascan_1"))
    placed = (P(SCAN, None, ASCAN, None), P(SCAN, ASCAN), P(SCAN, ASCAN))
    return jax.shard_map(
        body,
        mesh=finer,
        in_specs=placed,
        out_specs=(P(SCAN, ASCAN, None), P(SCAN, ASCAN, None), P(SCAN, ASCAN, None), P()),
        check_vma=False,
    )
```

profile of v0, /device:TPU:32, one launch (start us, length us, event | category | flops | bytes accessed | tf_op | source)
XLA Modules:
  0.0 195.4 jit_solution(9773354645260711611)
XLA Ops:
  0.7 8.7 %multiply_convert_fusion.1 = (bf16[512,1024]{1,0:T(8,128)(2,1)S(1)}, bf16[512,1024]{1,0:T(8,128)(2,1)S(1)}) fusion(f32[512]{0:T(512)S(1)} %sine_multiply_fusion), kind=kLoop, calls=%fused_computation.33 | loop fusion | flops 9437184 | bytes 2099200 | tf_op jit(solution)/shard_map/convert
  9.3 0.0 copy-start.2
  9.4 0.0 copy-start.4
  9.4 8.2 %reshape.54 = bf16[1024,4,512]{2,1,0:T(4,128)(2,1)} reshape(bf16[2,4,128,2048]{3,2,1,0:T(8,128)(2,1)} %param.3) | data formatting | bytes 8388608 | tf_op jit(solution)/shard_map/reshape | solution.py:57
  17.6 14.7 %fusion.36 = (bf16[1024,1,512]{2,1,0:T(2,128)(2,1)S(1)}, bf16[1024,1,512]{2,1,0:T(2,128)(2,1)}, bf16[1024,1,512]{2,1,0:T(2,128)(2,1)}, bf16[1024,1,512]{2,1,0:T(2,128)(2,1)S(1)}) fusion(bf16[1024,4,512]{2,1,0:T(4,128)(2,1)} %reshape.54), kind=kLoop, calls=%fused_computation.75 | loop fusion | bytes 8388608 | tf_op jit(solution)/shard_map/slice | solution.py:62
  32.4 2.3 %fusion.23 = f32[2048,1024]{0,1:T(8,128)S(1)} fusion(bf16[1024,1,512]{2,1,0:T(2,128)(2,1)S(1)} %get-tuple-element.25, bf16[512,1024]{1,0:T(8,128)(2,1)S(1)} %get-tuple-element.42, bf16[512,1024]{1,0:T(8,128)(2,1)S(1)} %get-tuple-element.41), kind=kOutput, calls=%fused_computation.52 | convolution fusion | flops 2151677952 | bytes 11534336 | tf_op jit(solution)/shard_map/dot_general | solution.py:62
  34.7 0.0 copy-done.2
  34.7 0.0 copy-done.4
  34.7 2.3 %fusion.20 = f32[2048,1024]{0,1:T(8,128)S(1)} fusion(bf16[1024,1,512]{2,1,0:T(2,128)(2,1)S(1)} %get-tuple-element.22, bf16[512,1024]{1,0:T(8,128)(2,1)S(1)} %get-tuple-element.42, bf16[512,1024]{1,0:T(8,128)(2,1)S(1)} %get-tuple-element.41), kind=kOutput, calls=%fused_computation.49 | convolution fusion | flops 2151677952 | bytes 11534336 | tf_op jit(solution)/shard_map/dot_general | solution.py:62
  37.1 4.9 %fusion.28 = (f32[2,128,1024]{2,1,0:T(8,128)}, f32[2,4,128,1024]{3,2,1,0:T(8,128)S(1)}, f32[2,128,1024]{2,1,0:T(8,128)}, f32[2,4,128,1024]{3,2,1,0:T(8,128)S(1)}) fusion(f32[2,4,128,2048]{3,2,1,0:T(8,128)S(1)} %bitcast.56, f32[2,4,128,2048]{3,2,1,0:T(8,128)S(1)} %bitcast.55), kind=kLoop, calls=%fused_computation.71 | loop fusion | flops 7864320 | bytes 27262976 | tf_op jit(solution)/shard_map/reduce_sum | solution.py:71
  42.0 0.9 divide_reduce_fusion.2
  42.8 0.0 copy-start.1
  42.8 0.0 copy-start.3
  42.9 0.0 copy-start.5
  42.9 0.9 divide_reduce_fusion.3
  43.7 0.7 copy-done.1
  44.4 0.3 copy-done.3
  44.7 0.3 copy-done.5
  45.0 2.3 %fusion.14 = f32[2048,1024]{0,1:T(8,128)S(1)} fusion(bf16[1024,1,512]{2,1,0:T(2,128)(2,1)S(1)} %copy-done.1, bf16[512,1024]{1,0:T(8,128)(2,1)S(1)} %copy-done.5, bf16[512,1024]{1,0:T(8,128)(2,1)S(1)} %copy-done.3), kind=kOutput, calls=%fused_computation.43 | convolution fusion | flops 2151677952 | bytes 11534336 | tf_op jit(solution)/shard_map/dot_general | solution.py:62
  47.4 0.0 copy-done
  47.4 5.6 %fusion.17 = f32[2048,1024]{0,1:T(8,128)} fusion(bf16[1024,1,512]{2,1,0:T(2,128)(2,1)S(1)} %copy-done, bf16[512,1024]{1,0:T(8,128)(2,1)S(1)} %copy-done.5, bf16[512,1024]{1,0:T(8,128)(2,1)S(1)} %copy-done.3), kind=kOutput, calls=%fused_computation.46 | convolution fusion | flops 2151677952 | bytes 11534336 | tf_op jit(solution)/shard_map/dot_general | solution.py:62
  52.9 7.3 %fusion.32 = (f32[2,128,1024]{2,1,0:T(8,128)}, f32[2,4,128,1024]{3,2,1,0:T(8,128)S(1)}, f32[2,128,1024]{2,1,0:T(8,128)}, f32[2,4,128,1024]{3,2,1,0:T(8,128)S(1)}) fusion(f32[2,4,128,2048]{3,2,1,0:T(8,128)} %bitcast.54, f32[2,4,128,2048]{3,2,1,0:T(8,128)S(1)} %bitcast.53), kind=kLoop, calls=%fused_computation.73 | loop fusion | flops 7864320 | bytes 27262976 | tf_op jit(solution)/shard_map/reduce_sum | solution.py:71
  60.2 0.9 divide_reduce_fusion
  61.1 0.0 copy-start.6
  61.1 0.0 copy-start.7
  61.1 0.9 divide_reduce_fusion.1
  62.0 0.0 copy-done.6
  62.0 0.0 copy-done.7
  62.0 4.1 %fusion.27 = (f32[]{:T(128)}, f32[2,128,1024]{2,1,0:T(8,128)S(1)}, f32[]{:T(128)}, f32[2,128,1024]{2,1,0:T(8,128)S(1)}, f32[2,128,1024]{2,1,0:T(8,128)S(1)}, /*i...) fusion(f32[2,128,1024]{2,1,0:T(8,128)S(1)} %divide_reduce_fusion, ...), kind=kLoop, calls=%fused_computation.70 | loop fusion | flops 5505022 | bytes 14682120 | tf_op jit(solution)/shard_map/reduce_sum | solution.py:81
  66.2 0.7 multiply_reduce_fusion.2
  66.9 0.7 multiply_reduce_fusion.3
  67.5 0.7 multiply_reduce_fusion.1
  68.2 0.7 multiply_reduce_fusion
  68.9 0.4 multiply_select_fusion
  69.3 0.2 pad_maximum_fusion
  69.5 3.5 %copy.18 = f32[6,128,1024]{1,0,2:T(8,128)} copy(f32[6,128,1024]{2,1,0:T(8,128)S(1)} %pad_maximum_fusion) | data formatting | bytes 6291456 | tf_op jit(solution)/shard_map/concatenate | solution.py:31
  73.0 11.2 %all-to-all-start = ((f32[6,128,1024]{1,0,2:T(8,128)}), f32[6,128,1024]{1,0,2:T(8,128)}, u32[]{:S(2)}, u32[]{:S(2)}) async-start(f32[6,128,1024]{1,0,2:T(8,128)} %copy.18), calls=%async_computation | async-start | bytes 8388608 | tf_op jit(solution)/shard_map/all_to_all | solution.py:33
  84.3 11.4 %all-reduce.3 = (f32[]{:T(128)}, f32[]{:T(128)}) all-reduce(f32[]{:T(128)} %get-tuple-element.12, f32[]{:T(128)} %get-tuple-element.35), channel_id=1, replica_groups=mesh['scan_0'=4,'scan_1'=2,'ascan_0'=4,'ascan_1'=8] {'scan_0'}, use_global_device_ids=true, to_apply=%region_13.14 | all-reduce | flops 2 | bytes 16 | tf_op jit(solution)/shard_map/psum | solution.py:26
  95.7 3.1 %all-reduce.4 = (f32[]{:T(128)}, f32[]{:T(128)}) all-reduce(f32[]{:T(128)} %get-tuple-element.8, f32[]{:T(128)} %get-tuple-element.9), channel_id=1, replica_groups=mesh['scan_0'=4,'scan_1'=2,'ascan_0'=4,'ascan_1'=8] {'scan_1'}, use_global_device_ids=true, to_apply=%region_14.15 | all-reduce | flops 2 | bytes 16 | tf_op jit(solution)/shard_map/psum | solution.py:26
  98.7 11.2 %all-reduce.2 = (f32[]{:T(128)}, f32[]{:T(128)}) all-reduce(f32[]{:T(128)} %get-tuple-element.10, f32[]{:T(128)} %get-tuple-element.11), channel_id=1, replica_groups=mesh['scan_0'=4,'scan_1'=2,'ascan_0'=4,'ascan_1'=8] {'ascan_0'}, use_global_device_ids=true, to_apply=%region_15.16 | all-reduce | flops 2 | bytes 16 | tf_op jit(solution)/shard_map/psum | solution.py:26
  109.9 76.1 %all-reduce.1 = (f32[]{:T(128)}, f32[]{:T(128)}) all-reduce(f32[]{:T(128)} %get-tuple-element.6, f32[]{:T(128)} %get-tuple-element.7), channel_id=1, replica_groups=mesh['scan_0'=4,'scan_1'=2,'ascan_0'=4,'ascan_1'=8] {'ascan_1'}, use_global_device_ids=true, to_apply=%region_16.17 | all-reduce | flops 2 | bytes 16 | tf_op jit(solution)/shard_map/psum | solution.py:26
  187.4 0.0 all-to-all-done
  187.4 2.8 %copy.19 = f32[6,128,1024]{1,2,0:T(8,128)S(1)} copy(f32[6,128,1024]{1,0,2:T(8,128)} %all-to-all-done) | data formatting | bytes 6291456 | tf_op jit(solution)/shard_map/all_to_all | solution.py:33
  190.2 0.4 slice_bitcast_fusion
  190.5 0.1 copy.51
  190.6 1.0 copy.49
  191.7 1.0 copy.50
  192.7 1.6 divide_bitcast_fusion
  (3 shorter events, 0.1 us)
Async XLA Ops:
  9.3 25.4 %copy-start.2 = (bf16[512,1024]{1,0:T(8,128)(2,1)}, bf16[512,1024]{1,0:T(8,128)(2,1)S(1)}, u32[]{:S(2)}) copy-start(bf16[512,1024]{1,0:T(8,128)(2,1)S(1)} %get-tuple-element.41) | copy-start | bytes 3145732
  9.4 25.4 %copy-start.4 = (bf16[512,1024]{1,0:T(8,128)(2,1)}, bf16[512,1024]{1,0:T(8,128)(2,1)S(1)}, u32[]{:S(2)}) copy-start(bf16[512,1024]{1,0:T(8,128)(2,1)S(1)} %get-tuple-element.42) | copy-start | bytes 3145732
  42.8 1.6 copy-start.1
  42.8 1.8 copy-start.3
  42.9 2.1 %copy-start.5 = (bf16[512,1024]{1,0:T(8,128)(2,1)S(1)}, bf16[512,1024]{1,0:T(8,128)(2,1)}, u32[]{:S(2)}) copy-start(bf16[512,1024]{1,0:T(8,128)(2,1)} %copy-done.4) | copy-start | bytes 3145732
  45.0 2.3 %copy-start = (bf16[1024,1,512]{2,1,0:T(2,128)(2,1)S(1)}, bf16[1024,1,512]{2,1,0:T(2,128)(2,1)}, u32[]{:S(2)}) copy-start(bf16[1024,1,512]{2,1,0:T(2,128)(2,1)} %get-tuple-element.24) | copy-start | bytes 3145732
  61.1 0.9 copy-start.6
  61.1 0.9 copy-start.7
  73.0 114.3 %all-to-all-start = ((f32[6,128,1024]{1,0,2:T(8,128)}), f32[6,128,1024]{1,0,2:T(8,128)}, u32[]{:S(2)}, u32[]{:S(2)}) async-start(f32[6,128,1024]{1,0,2:T(8,128)} %copy.18), calls=%async_computation | async-start | bytes 8388608 | tf_op jit(solution)/shard_map/all_to_all | solution.py:33
where the time goes:
time: 198 us; the launch traced here: 195 us
  blocking collectives  102 us (52%)
  other arithmetic  33.4 us (17%)
  local copies, waits for them, and re-layouts  33.1 us (17%)
  matrix products  12.6 us (6%)
  starting transfers between devices  11.2 us (6%)
  between operations  3.33 us (2%)
    psum x4, blocking collectives, over_axes(): value = lax.psum(value, axis)  102 us
    slice x1, local copies, waits for them, and re-layouts, band_moments(): flat[:, band_index, :]  14.7 us
    dot_general x4, matrix products, band_moments(): jnp.dot(flat[:, band_index, :], table_part, preferred_element_type=jnp.fl...  12.6 us
    reduce_sum x2, other arithmetic, band_moments(): amplitude_total = amplitude_total + jnp.sum(amplitude, axis=1)  12.2 us
    all_to_all x1, starting transfers between devices, in_one_piece(): lax.all_to_all(both, axis, split_axis=split_dim, concat_axis=concat_dim,...  11.2 us
    another operation x1, other arithmetic  8.66 us
    reshape x1, local copies, waits for them, and re-layouts, band_moments(): spectra.reshape(scan_count * repeat_count * ascan_count, BANDS, BAND_BINS)  8.24 us
    reduce_sum x1, other arithmetic, band_moments(): jnp.sum(decorrelation)  4.13 us
  transfers between devices with their start and end apart: 1, of which 0 were waited for; matrix products, arithmetic and copies ran while one was open for 0% of the time, Pallas kernels for 0%

commit v1 on v0

v1 whole, which is shorter than its diff:
```python
import functools
import math

import jax
import jax.numpy as jnp
import numpy as np
from jax import lax
from jax.experimental import pallas as pl
from jax.experimental.pallas import tpu as pltpu
from jax.sharding import PartitionSpec as P

REPEATS = 4
BINS = 2048
BANDS = 4
TILE = 128
BAND_BINS = 512
DEPTH = 1024
TILES = DEPTH // TILE
FLOOR = 0.05 * BAND_BINS
VARIANCE_SCALE = 0.1
TINY = float(np.finfo(np.float32).tiny)

MESH = pl.DeviceIdType.MESH
CHUNK = 32


def make_table():
    sample = np.arange(BAND_BINS, dtype=np.int32)
    depth = np.arange(DEPTH, dtype=np.int32)
    product = sample[:, None] * depth[None, :] % BINS
    angle = product.astype(np.float32) * np.float32(2.0 * math.pi / BINS)
    window = np.sin(np.float32(math.pi) * (sample.astype(np.float32) + np.float32(0.5)) / np.float32(BAND_BINS)) ** 2
    parts = np.stack([window[:, None] * np.cos(angle), window[:, None] * np.sin(angle)])
    parts = parts.reshape(2, BAND_BINS, TILES, TILE).transpose(2, 1, 0, 3)
    return jnp.asarray(parts.reshape(TILES, BAND_BINS, 2 * TILE), dtype=jnp.bfloat16)


def exchange_kernel(
    n_scan, n_ascan, scans, slab,
    spectra_ref, table_ref, top_ref, bottom_ref,
    maps_ref, stat_ref,
    profile, moments, outbox, flow, own_stat, line_stat, stat_a, stat_b,
    send_sem, recv_sem, own_sem, send_a, recv_a, send_b, recv_b,
):
    my_scan = lax.axis_index("scan")
    me = lax.axis_index("ascan")
    per_tile = TILE // slab

    barrier = pltpu.get_barrier_semaphore()

    @pl.loop(1, n_ascan)
    def _(d):
        pl.semaphore_signal(barrier, inc=1, device_id=(my_scan, lax.rem(me + d, n_ascan)), device_id_type=MESH)

    @pl.loop(1, n_scan)
    def _(d):
        pl.semaphore_signal(barrier, inc=1, device_id=(lax.rem(my_scan + d, n_scan), me), device_id_type=MESH)

    pl.semaphore_wait(barrier, n_ascan + n_scan - 2)

    flow[...] = jnp.zeros_like(flow)
    first_tile = me // per_tile

    def block_copy(tile, q, s, source, to):
        return pltpu.make_async_remote_copy(
            src_ref=outbox.at[tile, q, s],
            dst_ref=maps_ref.at[:, s, :, pl.ds(pl.multiple_of(source * TILE, TILE), TILE)],
            send_sem=send_sem.at[tile * per_tile + q, s],
            recv_sem=recv_sem.at[source, s],
            device_id=(my_scan, to),
            device_id_type=MESH,
        )

    def own_copy(s):
        return pltpu.make_async_copy(
            outbox.at[me // per_tile, lax.rem(me, per_tile), s],
            maps_ref.at[:, s, :, pl.ds(pl.multiple_of(me * TILE, TILE), TILE)],
            own_sem.at[s],
        )

    @pl.loop(0, TILES * scans)
    def _(step):
        tile = lax.rem(first_tile + 1 + step // scans, TILES)
        s = lax.rem(step, scans)
        table = table_ref[tile]
        for band in range(BANDS):
            rows = spectra_ref[s, :, :, band * BAND_BINS : (band + 1) * BAND_BINS]
            profile[band] = jnp.dot(
                rows.reshape(REPEATS * TILE, BAND_BINS), table, preferred_element_type=jnp.float32
            )

        @pl.loop(0, TILE // CHUNK)
        def _(chunk):
            similarity = jnp.zeros((CHUNK, TILE), jnp.float32)
            total = jnp.zeros((CHUNK, TILE), jnp.float32)
            near = jnp.zeros((CHUNK, TILE), jnp.float32)
            far = jnp.zeros((CHUNK, TILE), jnp.float32)
            for band in range(BANDS):
                power, amplitude = [], []
                for r in range(REPEATS):
                    at = pl.ds(pl.multiple_of(r * TILE + chunk * CHUNK, CHUNK), CHUNK)
                    c = profile[band, at, :TILE]
                    v = profile[band, at, TILE:]
                    p = c * c + v * v
                    power.append(p)
                    amplitude.append(p * lax.rsqrt(jnp.maximum(p, TINY)))
                for r in range(REPEATS - 1):
                    root = lax.rsqrt(jnp.maximum(power[r] + power[r + 1], FLOOR))
                    similarity += (amplitude[r] * root) * (amplitude[r + 1] * root)
                first = amplitude[0] + amplitude[1]
                second = amplitude[2] + amplitude[3]
                total += first + second
                d0 = amplitude[0] - amplitude[1]
                d1 = amplitude[2] - amplitude[3]
                d2 = first - second
                near += d0 * d0 + d1 * d1
                far += d2 * d2
            at = pl.ds(pl.multiple_of(chunk * CHUNK, CHUNK), CHUNK)
            moments[0, at, :] = 1.0 - similarity * (2.0 / (BANDS * (REPEATS - 1)))
            moments[1, at, :] = total * (1.0 / (BANDS * REPEATS * math.sqrt(BAND_BINS)))
            moments[2, at, :] = (near * 0.5 + far * 0.25) * (
                1.0 / (REPEATS * BANDS * VARIANCE_SCALE * BAND_BINS)
            )

        top = top_ref[pl.ds(s, 1), :]
        bottom = bottom_ref[pl.ds(s, 1), :]
        inside = ((top <= tile) & (tile < bottom)).astype(jnp.float32)
        for m in range(3):
            turned = moments[m].T * inside
            if m == 0:
                flow[...] += jnp.sum(turned.reshape(TILE // 8, 8, TILE), axis=0)
            for q in range(per_tile):
                outbox[tile, q, s, m] = turned[q * slab : (q + 1) * slab]

        @pl.loop(0, per_tile)
        def _(q):
            to = tile * per_tile + q

            @pl.when(to != me)
            def _():
                block_copy(tile, q, s, me, to).start()

            @pl.when(to == me)
            def _():
                own_copy(s).start()

    own_stat[pl.ds(0, 8), :] = flow[...]
    rows = (bottom_ref[...] - top_ref[...]).astype(jnp.float32) * float(TILE)
    own_stat[pl.ds(8, 8), :] = jnp.concatenate([rows, jnp.zeros((8 - scans, TILE), jnp.float32)], axis=0)
    stat_a[my_scan] = own_stat[...]

    def a_copy(source, to, k):
        return pltpu.make_async_remote_copy(
            src_ref=own_stat, dst_ref=stat_a.at[source],
            send_sem=send_a.at[k], recv_sem=recv_a.at[source],
            device_id=(to, me), device_id_type=MESH,
        )

    def b_copy(source, to, k):
        return pltpu.make_async_remote_copy(
            src_ref=line_stat, dst_ref=stat_b.at[source],
            send_sem=send_b.at[k], recv_sem=recv_b.at[source],
            device_id=(my_scan, to), device_id_type=MESH,
        )

    @pl.loop(1, n_scan)
    def _(d):
        a_copy(my_scan, lax.rem(my_scan + d, n_scan), d).start()

    @pl.loop(1, n_scan)
    def _(d):
        a_copy(lax.rem(my_scan + d, n_scan), lax.rem(my_scan + d, n_scan), d).wait_recv()

    line_stat[...] = jnp.sum(stat_a[...], axis=0)
    stat_b[me] = line_stat[...]

    @pl.loop(1, n_ascan)
    def _(d):
        b_copy(me, lax.rem(me + d, n_ascan), d).start()

    @pl.loop(1, n_scan)
    def _(d):
        a_copy(my_scan, lax.rem(my_scan + d, n_scan), d).wait_send()

    for s in range(scans):
        own_copy(s).wait()

    @pl.loop(1, n_ascan)
    def _(d):
        other = lax.rem(me + d, n_ascan)
        b_copy(other, other, d).wait_recv()
        for s in range(scans):
            block_copy(other // per_tile, lax.rem(other, per_tile), s, other, other).wait_recv()

    stat_ref[...] = jnp.sum(stat_b[...], axis=0)

    @pl.loop(1, n_ascan)
    def _(d):
        other = lax.rem(me + d, n_ascan)
        b_copy(me, other, d).wait_send()
        for s in range(scans):
            block_copy(other // per_tile, lax.rem(other, per_tile), s, me, other).wait_send()


def finish_kernel(maps_ref, stat_ref, angiogram_ref, structure_ref, speckle_ref, mean_ref):
    flow = jnp.sum(stat_ref[pl.ds(0, 8), :], keepdims=True)
    count = jnp.sum(stat_ref[pl.ds(8, 8), :], keepdims=True)
    mean = flow / count
    x = maps_ref[0, 0]
    width = x.shape[1]
    lane = lax.broadcasted_iota(jnp.int32, x.shape, 1)
    before = jnp.where(lane == 0, 0.0, pltpu.roll(x, 1, 1))
    after = jnp.where(lane == width - 1, 0.0, pltpu.roll(x, width - 1, 1))
    angiogram_ref[0] = (before + x + after) * (1.0 / (3.0 * mean))
    structure_ref[0] = maps_ref[1, 0]
    speckle_ref[0] = maps_ref[2, 0]
    mean_ref[...] = mean


def solution(mesh):
    n_scan, n_ascan = mesh.shape["scan"], mesh.shape["ascan"]

    def body(spectra, top, bottom):
        scans, repeats, lines, bins = spectra.shape
        slab = DEPTH // n_ascan
        width = lines * n_ascan
        f32 = jnp.float32
        vmem = pl.BlockSpec(memory_space=pltpu.VMEM)
        maps, stat = pl.pallas_call(
            functools.partial(exchange_kernel, n_scan, n_ascan, scans, slab),
            out_shape=(
                jax.ShapeDtypeStruct((3, scans, slab, width), f32),
                jax.ShapeDtypeStruct((16, TILE), f32),
            ),
            in_specs=[vmem] * 4,
            out_specs=(pl.BlockSpec(memory_space=pl.ANY), vmem),
            scratch_shapes=[
                pltpu.VMEM((BANDS, REPEATS * TILE, 2 * TILE), f32),
                pltpu.VMEM((3, TILE, TILE), f32),
                pltpu.VMEM((TILES, TILE // slab, scans, 3, slab, TILE), f32),
                pltpu.VMEM((8, TILE), f32),
                pltpu.VMEM((16, TILE), f32),
                pltpu.VMEM((16, TILE), f32),
                pltpu.VMEM((n_scan, 16, TILE), f32),
                pltpu.VMEM((n_ascan, 16, TILE), f32),
                pltpu.SemaphoreType.DMA((n_ascan, scans)),
                pltpu.SemaphoreType.DMA((n_ascan, scans)),
                pltpu.SemaphoreType.DMA((scans,)),
                pltpu.SemaphoreType.DMA((n_scan,)),
                pltpu.SemaphoreType.DMA((n_scan,)),
                pltpu.SemaphoreType.DMA((n_ascan,)),
                pltpu.SemaphoreType.DMA((n_ascan,)),
            ],
            compiler_params=pltpu.CompilerParams(
                collective_id=0, has_side_effects=True, vmem_limit_bytes=32 * 2**20
            ),
            name="exchange",
        )(spectra, make_table(), top, bottom)

        block = 16
        out_spec = pl.BlockSpec((1, block, width), lambda s, k: (s, k, 0))
        angiogram, structure, speckle, mean = pl.pallas_call(
            finish_kernel,
            grid=(scans, slab // block),
            out_shape=[jax.ShapeDtypeStruct((scans, slab, width), f32)] * 3
            + [jax.ShapeDtypeStruct((1, 1), f32)],
            in_specs=[
                pl.BlockSpec((3, 1, block, width), lambda s, k: (0, s, k, 0)),
                pl.BlockSpec((16, TILE), lambda s, k: (0, 0)),
            ],
            out_specs=[out_spec] * 3 + [pl.BlockSpec((1, 1), lambda s, k: (0, 0))],
            name="finish",
        )(maps, stat)
        return angiogram, structure, speckle, mean.reshape(())

    return jax.shard_map(
        body,
        mesh=mesh,
        in_specs=(P("scan", None, "ascan", None), P("scan", "ascan"), P("scan", "ascan")),
        out_specs=(P("scan", "ascan", None),) * 3 + (P(),),
        check_vma=False,
    )
```

time: 198 us -> 103 us (0.52)
  blocking collectives: 102 us -> 0 us
  Pallas kernels: 0 us -> 93 us
  other arithmetic: 33.4 us -> 0 us
  local copies, waits for them, and re-layouts: 33.1 us -> 7.36 us
  matrix products: 12.6 us -> 0 us
  starting transfers between devices: 11.2 us -> 0 us
  between operations: 3.33 us -> 0.66 us
    psum x4 -> x0, blocking collectives: 102 us -> none  [over_axes(): value = lax.psum(value, axis)]
    pallas_call x0 -> x2, Pallas kernels: none -> 93 us  [the longest x1 88.6 us: body(): pl.pallas_call(functools.partial(exchange_kernel, n_scan, n_ascan, scans,...]
    reduce_sum x11 -> x0, other arithmetic: 22.5 us -> none  [the longest x2 12.2 us: band_moments(): amplitude_total = amplitude_total + jnp.sum(amplitude, axis=1)]
    slice x4 -> x0, local copies, waits for them, and re-layouts: 16.9 us -> none  [the longest x1 14.7 us: band_moments(): flat[:, band_index, :]]
    dot_general x4 -> x0, matrix products: 12.6 us -> none  [band_moments(): jnp.dot(flat[:, band_index, :], table_part, preferred_element_type=jnp.fl...]
    all_to_all x1 -> x0, starting transfers between devices: 11.2 us -> none  [in_one_piece(): lax.all_to_all(both, axis, split_axis=split_dim, concat_axis=concat_dim,...]
    another operation x1 -> x0, other arithmetic: 8.66 us -> none
    reshape x1 -> x0, local copies, waits for them, and re-layouts: 8.24 us -> none  [band_moments(): spectra.reshape(scan_count * repeat_count * ascan_count, BANDS, BAND_BINS)]
  transfers between devices with their start and end apart: 1 -> 0, of which waited for: 0 -> 0; matrix products, arithmetic and copies ran while one was open for 0% -> 0% of each run, Pallas kernels for 0% -> 0%
where the time goes in v1:
time: 103 us; the launch traced here: 101 us
  Pallas kernels  93 us (90%)
  local copies, waits for them, and re-layouts  7.36 us (7%)
    pallas_call x1, Pallas kernels, body(): pl.pallas_call(functools.partial(exchange_kernel, n_scan, n_ascan, scans,...  88.6 us
    unnamed x12, local copies, waits for them, and re-layouts  7.36 us
    pallas_call x1, Pallas kernels, body(): pl.pallas_call(finish_kernel, grid=(scans, slab // block), out_shape=[jax...  4.41 us

profile of v1, /device:TPU:32, one launch (start us, length us, event | category | flops | bytes accessed | tf_op | source)
XLA Modules:
  0.0 101.1 jit_solution(7806890268501198739)
XLA Ops:
  0.6 0.0 copy-start
  0.6 2.2 %copy-done = bf16[2,4,128,2048]{3,2,1,0:T(8,128)(2,1)S(1)} copy-done((bf16[2,4,128,2048]{3,2,1,0:T(8,128)(2,1)S(1)}, bf16[2,4,128,2048]{3,2,1,0:T(8,128)(2,1)}, u32[]{:S(2)}) %copy-start) | copy-done | bytes 4194328
  2.8 0.0 copy-start.2
  2.8 1.6 %copy-done.2 = bf16[8,512,256]{2,1,0:T(8,128)(2,1)S(1)} copy-done((bf16[8,512,256]{2,1,0:T(8,128)(2,1)S(1)}, bf16[8,512,256]{2,1,0:T(8,128)(2,1)}, u32[]{:S(2)}) %copy-start.2) | copy-done | bytes 2097176
  4.4 0.0 copy-start.4
  4.4 0.7 copy-done.4
  5.1 0.0 copy-start.5
  5.1 0.7 copy-done.5
  5.8 88.6 %exchange.1 = (f32[3,2,32,4096]{3,2,1,0:T(8,128)S(1)}, f32[16,128]{1,0:T(8,128)S(1)}) custom-call(bf16[2,4,128,2048]{3,2,1,0:T(8,128)(2,1)S(1)} %copy-done, bf16[8,512,256]{2,1,0:T(8,128)(2,1)S(1)} %copy-done.2, s32[2,128]{1,0:T(2,128)S(1)} %copy-done.4, s32[2,128]{1,0:T(2,128)S(1)} %copy-done.5), custom_call_target="tpu_custom_call" | custom-call | tf_op jit(solution)/shard_map/exchange/pallas_call | solution.py:229
  94.4 0.0 copy-start.1
  94.4 1.6 %copy-done.1 = f32[3,2,32,4096]{3,2,1,0:T(8,128)} copy-done((f32[3,2,32,4096]{3,2,1,0:T(8,128)}, f32[3,2,32,4096]{3,2,1,0:T(8,128)S(1)}, u32[]{:S(2)}) %copy-start.1) | copy-done | bytes 3145752
  96.1 0.0 copy-start.3
  96.1 0.6 copy-done.3
  96.6 4.4 %finish.1 = (f32[2,32,4096]{2,1,0:T(8,128)}, f32[2,32,4096]{2,1,0:T(8,128)}, f32[2,32,4096]{2,1,0:T(8,128)}, f32[1,1]{1,0:T(1,128)}) custom-call(f32[3,2,32,4096]{3,2,1,0:T(8,128)} %copy-done.1, f32[16,128]{1,0:T(8,128)} %copy-done.3), custom_call_target="tpu_custom_call" | custom-call | tf_op jit(solution)/shard_map/finish/pallas_call | solution.py:262
Async XLA Ops:
  0.6 2.2 %copy-start = (bf16[2,4,128,2048]{3,2,1,0:T(8,128)(2,1)S(1)}, bf16[2,4,128,2048]{3,2,1,0:T(8,128)(2,1)}, u32[]{:S(2)}) copy-start(bf16[2,4,128,2048]{3,2,1,0:T(8,128)(2,1)} %spectra_ref.1) | copy-start | bytes 12582916
  2.8 1.6 %copy-start.2 = (bf16[8,512,256]{2,1,0:T(8,128)(2,1)S(1)}, bf16[8,512,256]{2,1,0:T(8,128)(2,1)}, u32[]{:S(2)}) copy-start(bf16[8,512,256]{2,1,0:T(8,128)(2,1)} %constant.2.clone.table_ref) | copy-start | bytes 6291460
  4.4 0.7 copy-start.4
  5.1 0.7 copy-start.5
  94.4 1.6 %copy-start.1 = (f32[3,2,32,4096]{3,2,1,0:T(8,128)}, f32[3,2,32,4096]{3,2,1,0:T(8,128)S(1)}, u32[]{:S(2)}) copy-start(f32[3,2,32,4096]{3,2,1,0:T(8,128)S(1)} %get-tuple-element.10.maps_ref) | copy-start | bytes 9437188
  96.1 0.6 copy-start.3

commit v2 on v1

v2 whole, which is shorter than its diff:
```python
import functools
import math

import jax
import jax.numpy as jnp
import numpy as np
from jax import lax
from jax.experimental import pallas as pl
from jax.experimental.pallas import tpu as pltpu
from jax.sharding import PartitionSpec as P

REPEATS = 4
BINS = 2048
BANDS = 4
TILE = 128
BAND_BINS = 512
DEPTH = 1024
TILES = DEPTH // TILE
FLOOR = 0.05 * BAND_BINS
VARIANCE_SCALE = 0.1
TINY = float(np.finfo(np.float32).tiny)

MESH = pl.DeviceIdType.MESH
CHUNK = 32


def make_table():
    sample = np.arange(BAND_BINS, dtype=np.int32)
    depth = np.arange(DEPTH, dtype=np.int32)
    product = sample[:, None] * depth[None, :] % BINS
    angle = product.astype(np.float32) * np.float32(2.0 * math.pi / BINS)
    window = np.sin(np.float32(math.pi) * (sample.astype(np.float32) + np.float32(0.5)) / np.float32(BAND_BINS)) ** 2
    parts = np.stack([window[:, None] * np.cos(angle), window[:, None] * np.sin(angle)])
    parts = parts.reshape(2, BAND_BINS, TILES, TILE).transpose(2, 1, 0, 3)
    return jnp.asarray(parts.reshape(TILES, BAND_BINS, 2 * TILE), dtype=jnp.bfloat16)


def exchange_kernel(
    n_scan, n_ascan, scans, slab,
    spectra_hbm, table_hbm, top_hbm, bottom_hbm,
    maps_ref, stat_ref,
    spectra, table, top_ref, bottom_ref, profile, sums, outbox, flow, own_stat, line_stat, stat_a, stat_b,
    spectra_sem, table_sem, surface_sem, send_sem, recv_sem, own_sem, send_a, recv_a, send_b, recv_b,
):
    my_scan = lax.axis_index("scan")
    me = lax.axis_index("ascan")
    per_tile = TILE // slab
    first_tile = lax.rem(me // per_tile + 1, TILES)

    barrier = pltpu.get_barrier_semaphore()

    @pl.loop(1, n_ascan)
    def _(d):
        pl.semaphore_signal(barrier, inc=1, device_id=(my_scan, lax.rem(me + d, n_ascan)), device_id_type=MESH)

    @pl.loop(1, n_scan)
    def _(d):
        pl.semaphore_signal(barrier, inc=1, device_id=(lax.rem(my_scan + d, n_scan), me), device_id_type=MESH)

    def table_copy(tile):
        return pltpu.make_async_copy(table_hbm.at[tile], table.at[tile], table_sem.at[tile])

    def spectra_copy(s, band):
        bins = pl.ds(band * BAND_BINS, BAND_BINS)
        return pltpu.make_async_copy(
            spectra_hbm.at[s, :, :, bins], spectra.at[s, band], spectra_sem.at[s, band]
        )

    surface_copies = (
        pltpu.make_async_copy(top_hbm, top_ref, surface_sem.at[0]),
        pltpu.make_async_copy(bottom_hbm, bottom_ref, surface_sem.at[1]),
    )
    table_copy(first_tile).start()
    for s in range(scans):
        for band in range(BANDS):
            spectra_copy(s, band).start()
        if s == 0:
            for c in surface_copies:
                c.start()

    @pl.loop(1, TILES)
    def _(d):
        table_copy(lax.rem(first_tile + d, TILES)).start()

    flow[...] = jnp.zeros_like(flow)

    def block_copy(tile, q, s, source, to):
        return pltpu.make_async_remote_copy(
            src_ref=outbox.at[tile, q, s],
            dst_ref=maps_ref.at[:, s, :, pl.ds(pl.multiple_of(source * TILE, TILE), TILE)],
            send_sem=send_sem.at[tile * per_tile + q, s],
            recv_sem=recv_sem.at[source, s],
            device_id=(my_scan, to),
            device_id_type=MESH,
        )

    def own_copy(s):
        return pltpu.make_async_copy(
            outbox.at[me // per_tile, lax.rem(me, per_tile), s],
            maps_ref.at[:, s, :, pl.ds(pl.multiple_of(me * TILE, TILE), TILE)],
            own_sem.at[s],
        )

    def band_terms(band, at):
        power, amplitude = [], []
        for r in range(REPEATS):
            rows = pl.ds(r * TILE + at, CHUNK)
            c = profile[band, rows, :TILE]
            v = profile[band, rows, TILE:]
            p = c * c + v * v
            power.append(p)
            amplitude.append(p * lax.rsqrt(jnp.maximum(p, TINY)))
        similarity = None
        for r in range(REPEATS - 1):
            root = lax.rsqrt(jnp.maximum(power[r] + power[r + 1], FLOOR))
            term = (amplitude[r] * root) * (amplitude[r + 1] * root)
            similarity = term if similarity is None else similarity + term
        first = amplitude[0] + amplitude[1]
        second = amplitude[2] + amplitude[3]
        d0 = amplitude[0] - amplitude[1]
        d1 = amplitude[2] - amplitude[3]
        d2 = first - second
        return similarity, first + second, (d0 * d0 + d1 * d1) + (d2 * d2) * 0.5

    @pl.loop(0, TILES * scans)
    def _(step):
        tile = lax.rem(first_tile + step // scans, TILES)
        s = lax.rem(step, scans)

        @pl.when(s == 0)
        def _():
            table_copy(tile).wait()

        @pl.when(step < scans)
        def _():
            for band in range(BANDS):
                spectra_copy(s, band).wait()

        weights = table[tile]
        for band in range(BANDS):
            profile[band] = jnp.dot(
                spectra[s, band].reshape(REPEATS * TILE, BAND_BINS),
                weights,
                preferred_element_type=jnp.float32,
            )
            for at in range(0, TILE, CHUNK):
                terms = band_terms(band, at)
                for m in range(3):
                    rows = pl.ds(at, CHUNK)
                    sums[m, rows, :] = terms[m] if band == 0 else sums[m, rows, :] + terms[m]

        @pl.when(step == 0)
        def _():
            for c in surface_copies:
                c.wait()

        top = top_ref[pl.ds(s, 1), :]
        bottom = bottom_ref[pl.ds(s, 1), :]
        inside = ((top <= tile) & (tile < bottom)).astype(jnp.float32)
        for m in range(3):
            turned = sums[m].T
            if m == 0:
                turned = (1.0 - turned * (2.0 / (BANDS * (REPEATS - 1)))) * inside
                flow[...] += jnp.sum(turned.reshape(TILE // 8, 8, TILE), axis=0)
            elif m == 1:
                turned = turned * (inside * (1.0 / (BANDS * REPEATS * math.sqrt(BAND_BINS))))
            else:
                turned = turned * (inside * (0.5 / (REPEATS * BANDS * VARIANCE_SCALE * BAND_BINS)))
            for q in range(per_tile):
                outbox[tile, q, s, m] = turned[q * slab : (q + 1) * slab]

        @pl.when(step == 0)
        def _():
            pl.semaphore_wait(barrier, n_ascan + n_scan - 2)

        @pl.loop(0, per_tile)
        def _(q):
            to = tile * per_tile + q

            @pl.when(to != me)
            def _():
                block_copy(tile, q, s, me, to).start()

            @pl.when(to == me)
            def _():
                own_copy(s).start()

    rows = jnp.sum((bottom_ref[...] - top_ref[...]).astype(jnp.float32), axis=0, keepdims=True)
    own_stat[pl.ds(0, 1), :] = jnp.sum(flow[...], axis=0, keepdims=True)
    own_stat[pl.ds(1, 1), :] = rows * float(TILE)
    stat_a[my_scan] = own_stat[...]

    def a_copy(source, to, k):
        return pltpu.make_async_remote_copy(
            src_ref=own_stat, dst_ref=stat_a.at[source],
            send_sem=send_a.at[k], recv_sem=recv_a.at[source],
            device_id=(to, me), device_id_type=MESH,
        )

    def b_copy(source, to, k):
        return pltpu.make_async_remote_copy(
            src_ref=line_stat, dst_ref=stat_b.at[source],
            send_sem=send_b.at[k], recv_sem=recv_b.at[source],
            device_id=(my_scan, to), device_id_type=MESH,
        )

    @pl.loop(1, n_scan)
    def _(d):
        a_copy(my_scan, lax.rem(my_scan + d, n_scan), d).start()

    @pl.loop(1, n_scan)
    def _(d):
        a_copy(lax.rem(my_scan + d, n_scan), lax.rem(my_scan + d, n_scan), d).wait_recv()

    line_stat[...] = jnp.sum(stat_a[...], axis=0)
    stat_b[me] = line_stat[...]

    @pl.loop(1, n_ascan)
    def _(d):
        b_copy(me, lax.rem(me + d, n_ascan), d).start()

    @pl.loop(1, n_scan)
    def _(d):
        a_copy(my_scan, lax.rem(my_scan + d, n_scan), d).wait_send()

    @pl.loop(1, n_ascan)
    def _(d):
        other = lax.rem(me + d, n_ascan)
        b_copy(other, other, d).wait_recv()

    stat_ref[...] = jnp.sum(stat_b[...], axis=0)
    for s in range(scans):
        own_copy(s).wait()

    @pl.loop(1, n_ascan)
    def _(d):
        other = lax.rem(me + d, n_ascan)
        b_copy(me, other, d).wait_send()
        for s in range(scans):
            block_copy(other // per_tile, lax.rem(other, per_tile), s, me, other).wait_send()

    @pl.loop(1, n_ascan)
    def _(d):
        other = lax.rem(me + d, n_ascan)
        for s in range(scans):
            block_copy(other // per_tile, lax.rem(other, per_tile), s, other, other).wait_recv()


def finish_kernel(maps_ref, stat_ref, angiogram_ref, structure_ref, speckle_ref, mean_ref, maps, smooth, sem_in, sem_out):
    scans, slab, width = angiogram_ref.shape
    outs = (angiogram_ref, structure_ref, speckle_ref)
    reads = [[pltpu.make_async_copy(maps_ref.at[m, s], maps.at[m, s], sem_in.at[m, s]) for s in range(scans)] for m in range(3)]
    writes = [
        [
            pltpu.make_async_copy(smooth.at[s] if m == 0 else maps.at[m, s], outs[m].at[s], sem_out.at[m, s])
            for s in range(scans)
        ]
        for m in range(3)
    ]
    for m in range(3):
        for s in range(scans):
            reads[m][s].start()
    totals = jnp.sum(stat_ref[...], axis=1, keepdims=True)
    mean = totals[0:1] / totals[1:2]
    scale = 1.0 / (3.0 * mean)
    mean_ref[...] = mean
    lane = lax.broadcasted_iota(jnp.int32, (8, width), 1)
    for s in range(scans):
        reads[0][s].wait()
        for z in range(0, slab, 8):
            x = maps[0, s, pl.ds(z, 8), :]
            before = jnp.where(lane == 0, 0.0, pltpu.roll(x, 1, 1))
            after = jnp.where(lane == width - 1, 0.0, pltpu.roll(x, width - 1, 1))
            smooth[s, pl.ds(z, 8), :] = (before + x + after) * scale
        writes[0][s].start()
        for m in (1, 2):
            reads[m][s].wait()
            writes[m][s].start()
    for m in range(3):
        for s in range(scans):
            writes[m][s].wait()


def solution(mesh):
    n_scan, n_ascan = mesh.shape["scan"], mesh.shape["ascan"]

    def body(spectra, top, bottom):
        scans, repeats, lines, bins = spectra.shape
        slab = DEPTH // n_ascan
        width = lines * n_ascan
        f32 = jnp.float32
        vmem = pl.BlockSpec(memory_space=pltpu.VMEM)
        hbm = pl.BlockSpec(memory_space=pltpu.HBM)
        maps, stat = pl.pallas_call(
            functools.partial(exchange_kernel, n_scan, n_ascan, scans, slab),
            out_shape=(
                jax.ShapeDtypeStruct((3, scans, slab, width), f32),
                jax.ShapeDtypeStruct((2, TILE), f32),
            ),
            in_specs=[hbm] * 4,
            out_specs=(hbm, vmem),
            scratch_shapes=[
                pltpu.VMEM((scans, BANDS, REPEATS, TILE, BAND_BINS), jnp.bfloat16),
                pltpu.VMEM((TILES, BAND_BINS, 2 * TILE), jnp.bfloat16),
                pltpu.VMEM((scans, TILE), jnp.int32),
                pltpu.VMEM((scans, TILE), jnp.int32),
                pltpu.VMEM((BANDS, REPEATS * TILE, 2 * TILE), f32),
                pltpu.VMEM((3, TILE, TILE), f32),
                pltpu.VMEM((TILES, TILE // slab, scans, 3, slab, TILE), f32),
                pltpu.VMEM((8, TILE), f32),
                pltpu.VMEM((2, TILE), f32),
                pltpu.VMEM((2, TILE), f32),
                pltpu.VMEM((n_scan, 2, TILE), f32),
                pltpu.VMEM((n_ascan, 2, TILE), f32),
                pltpu.SemaphoreType.DMA((scans, BANDS)),
                pltpu.SemaphoreType.DMA((TILES,)),
                pltpu.SemaphoreType.DMA((2,)),
                pltpu.SemaphoreType.DMA((n_ascan, scans)),
                pltpu.SemaphoreType.DMA((n_ascan, scans)),
                pltpu.SemaphoreType.DMA((scans,)),
                pltpu.SemaphoreType.DMA((n_scan,)),
                pltpu.SemaphoreType.DMA((n_scan,)),
                pltpu.SemaphoreType.DMA((n_ascan,)),
                pltpu.SemaphoreType.DMA((n_ascan,)),
            ],
            compiler_params=pltpu.CompilerParams(
                collective_id=0, has_side_effects=True, vmem_limit_bytes=58 * 2**20
            ),
            name="exchange",
        )(spectra, make_table(), top, bottom)

        angiogram, structure, speckle, mean = pl.pallas_call(
            finish_kernel,
            out_shape=[jax.ShapeDtypeStruct((scans, slab, width), f32)] * 3
            + [jax.ShapeDtypeStruct((1, 1), f32)],
            in_specs=[hbm, vmem],
            out_specs=[hbm] * 3 + [vmem],
            scratch_shapes=[
                pltpu.VMEM((3, scans, slab, width), f32),
                pltpu.VMEM((scans, slab, width), f32),
                pltpu.SemaphoreType.DMA((3, scans)),
                pltpu.SemaphoreType.DMA((3, scans)),
            ],
            name="finish",
        )(maps, stat)
        return angiogram, structure, speckle, mean.reshape(())

    return jax.shard_map(
        body,
        mesh=mesh,
        in_specs=(P("scan", None, "ascan", None), P("scan", "ascan"), P("scan", "ascan")),
        out_specs=(P("scan", "ascan", None),) * 3 + (P(),),
        check_vma=False,
    )
```

time: 103 us -> 91.2 us (0.89)
  local copies, waits for them, and re-layouts: 7.36 us -> 0 us
  Pallas kernels: 93 us -> 89.6 us
    unnamed x12 -> x0, local copies, waits for them, and re-layouts: 7.36 us -> none
    pallas_call x1, Pallas kernels: 88.6 us -> 85.1 us  [body(): pl.pallas_call(functools.partial(exchange_kernel, n_scan, n_ascan, scans,...]
where the time goes in v2:
time: 91.2 us; the launch traced here: 90.2 us
  Pallas kernels  89.6 us (98%)
    pallas_call x1, Pallas kernels, body(): pl.pallas_call(functools.partial(exchange_kernel, n_scan, n_ascan, scans,...  85.1 us
    pallas_call x1, Pallas kernels, body(): pl.pallas_call(finish_kernel, out_shape=[jax.ShapeDtypeStruct((scans, sla...  4.45 us

profile of v2, /device:TPU:32, one launch (start us, length us, event | category | flops | bytes accessed | tf_op | source)
XLA Modules:
  0.0 90.2 jit_solution(13004562948818080089)
XLA Ops:
  0.6 85.1 %exchange.1 = (f32[3,2,32,4096]{3,2,1,0:T(8,128)}, f32[2,128]{1,0:T(2,128)}) custom-call(bf16[2,4,128,2048]{3,2,1,0:T(8,128)(2,1)} %spectra_hbm.1, bf16[8,512,256]{2,1,0:T(8,128)(2,1)} %constant.2.clone.table_hbm, s32[2,128]{1,0:T(2,128)} %top_hbm.1, s32[2,128]{1,0:T(2,128)} %bottom_hbm.1), custom_call_target="tpu_custom_call" | custom-call | tf_op jit(solution)/shard_map/exchange/pallas_call | solution.py:294
  85.8 4.4 %finish.1 = (f32[2,32,4096]{2,1,0:T(8,128)}, f32[2,32,4096]{2,1,0:T(8,128)}, f32[2,32,4096]{2,1,0:T(8,128)}, f32[1,1]{1,0:T(1,128)}) custom-call(f32[3,2,32,4096]{3,2,1,0:T(8,128)} %get-tuple-element.10.maps_ref, f32[2,128]{1,0:T(2,128)} %get-tuple-element.11.stat_ref), custom_call_target="tpu_custom_call" | custom-call | tf_op jit(solution)/shard_map/finish/pallas_call | solution.py:332

commit v3 on v2

v3 whole, which is shorter than its diff:
```python
import functools
import math

import jax
import jax.numpy as jnp
import numpy as np
from jax import lax
from jax.experimental import pallas as pl
from jax.experimental.pallas import tpu as pltpu
from jax.sharding import PartitionSpec as P

REPEATS = 4
BINS = 2048
BANDS = 4
TILE = 128
BAND_BINS = 512
DEPTH = 1024
TILES = DEPTH // TILE
FLOOR = 0.05 * BAND_BINS
VARIANCE_SCALE = 0.1
TINY = float(np.finfo(np.float32).tiny)

MESH = pl.DeviceIdType.MESH
CHUNK = 32
SLAB = 32
RING = 8
HELD = 4


def make_table():
    sample = np.arange(BAND_BINS, dtype=np.int32)
    depth = np.arange(DEPTH, dtype=np.int32)
    product = sample[:, None] * depth[None, :] % BINS
    angle = product.astype(np.float32) * np.float32(2.0 * math.pi / BINS)
    window = np.sin(np.float32(math.pi) * (sample.astype(np.float32) + np.float32(0.5)) / np.float32(BAND_BINS)) ** 2
    parts = np.stack([window[:, None] * np.cos(angle), window[:, None] * np.sin(angle)])
    parts = parts.reshape(2, BAND_BINS, TILE // SLAB, RING, SLAB).transpose(3, 1, 0, 2, 4)
    return jnp.asarray(parts.reshape(RING, BAND_BINS, 2 * TILE), dtype=jnp.bfloat16)


def exchange_kernel(
    n_scan, n_ascan, scans, slab,
    spectra_hbm, table_hbm, top_hbm, bottom_hbm,
    maps_ref, stat_ref,
    spectra, table, top_ref, bottom_ref, profile, sums, outbox, flow, own_stat, line_stat, stat_a, stat_b,
    spectra_sem, table_sem, surface_sem, send_sem, recv_sem, send_a, recv_a, send_b, recv_b,
):
    my_scan = lax.axis_index("scan")
    me = lax.axis_index("ascan")
    per_tile = TILE // slab
    row, place = me // RING, lax.rem(me, RING)

    def group_of(step):
        pair = step // (2 * scans)
        reach = jnp.where(pair == 0, 2, jnp.where(pair == 1, 1, 3))
        near = jnp.where(lax.rem(step, 2) == 0, reach, RING - reach)
        distance = jnp.where(step < 6 * scans, near, jnp.where(step < 7 * scans, 4, 0))
        return lax.rem(place + distance, RING)

    def scan_of(step):
        return jnp.where(step < 6 * scans, lax.rem(step // 2, scans), lax.rem(step, scans))


    barrier = pltpu.get_barrier_semaphore()

    @pl.loop(1, n_ascan)
    def _(d):
        pl.semaphore_signal(barrier, inc=1, device_id=(my_scan, lax.rem(me + d, n_ascan)), device_id_type=MESH)

    @pl.loop(1, n_scan)
    def _(d):
        pl.semaphore_signal(barrier, inc=1, device_id=(lax.rem(my_scan + d, n_scan), me), device_id_type=MESH)

    def table_copy(tile):
        return pltpu.make_async_copy(table_hbm.at[tile], table.at[tile], table_sem.at[tile])

    def spectra_copy(s, band):
        bins = pl.ds(band * BAND_BINS, BAND_BINS)
        return pltpu.make_async_copy(
            spectra_hbm.at[s, :, :, bins], spectra.at[s, band], spectra_sem.at[s, band]
        )

    surface_copies = (
        pltpu.make_async_copy(top_hbm, top_ref, surface_sem.at[0]),
        pltpu.make_async_copy(bottom_hbm, bottom_ref, surface_sem.at[1]),
    )
    table_copy(group_of(0)).start()
    for s in range(scans):
        for band in range(BANDS):
            spectra_copy(s, band).start()
        if s == 0:
            for c in surface_copies:
                c.start()

    @pl.loop(1, RING)
    def _(d):
        table_copy(group_of(jnp.where(d < 6, d // 2 * (2 * scans) + lax.rem(d, 2), d * scans))).start()

    flow[...] = jnp.zeros_like(flow)

    def block_copy(s, source, to):
        return pltpu.make_async_remote_copy(
            src_ref=outbox.at[to, s],
            dst_ref=maps_ref.at[:, s, :, pl.ds(pl.multiple_of(source * TILE, TILE), TILE)],
            send_sem=send_sem.at[to, s],
            recv_sem=recv_sem.at[source, s],
            device_id=(my_scan, to),
            device_id_type=MESH,
        )

    def send(group, s):
        @pl.loop(0, per_tile)
        def _(d):
            to = lax.rem(row + d, per_tile) * RING + group

            @pl.when(to != me)
            def _():
                block_copy(s, me, to).start()

            @pl.when(to == me)
            def _():
                maps_ref[:, s, :, pl.ds(pl.multiple_of(me * TILE, TILE), TILE)] = outbox[me, s]

    def band_terms(band, at):
        power, amplitude = [], []
        for r in range(REPEATS):
            rows = pl.ds(r * TILE + at, CHUNK)
            c = profile[band, rows, :TILE]
            v = profile[band, rows, TILE:]
            p = c * c + v * v
            power.append(p)
            amplitude.append(p * lax.rsqrt(jnp.maximum(p, TINY)))
        similarity = None
        for r in range(REPEATS - 1):
            root = lax.rsqrt(jnp.maximum(power[r] + power[r + 1], FLOOR))
            term = (amplitude[r] * root) * (amplitude[r + 1] * root)
            similarity = term if similarity is None else similarity + term
        first = amplitude[0] + amplitude[1]
        second = amplitude[2] + amplitude[3]
        d0 = amplitude[0] - amplitude[1]
        d1 = amplitude[2] - amplitude[3]
        d2 = first - second
        return similarity, first + second, (d0 * d0 + d1 * d1) + (d2 * d2) * 0.5

    @pl.loop(0, RING * scans)
    def _(step):
        group, s = group_of(step), scan_of(step)

        @pl.when(s == 0)
        def _():
            table_copy(group).wait()

        @pl.when((step == 0) | (step == 2))
        def _():
            for band in range(BANDS):
                spectra_copy(s, band).wait()

        weights = table[group]
        for band in range(BANDS):

            profile[band] = jnp.dot(
                spectra[s, band].reshape(REPEATS * TILE, BAND_BINS),
                weights,
                preferred_element_type=jnp.float32,
            )
            for at in range(0, TILE, CHUNK):
                terms = band_terms(band, at)
                for m in range(3):
                    rows = pl.ds(at, CHUNK)
                    sums[m, rows, :] = terms[m] if band == 0 else sums[m, rows, :] + terms[m]

        @pl.when(step == 0)
        def _():
            for c in surface_copies:
                c.wait()

        top = top_ref[pl.ds(s, 1), :]
        bottom = bottom_ref[pl.ds(s, 1), :]
        masks = []
        for q in range(per_tile):
            tile = (q * RING + group) * slab // TILE
            masks.append(((top <= tile) & (tile < bottom)).astype(jnp.float32))
        for m in range(3):
            turned = sums[m].T
            for q in range(per_tile):
                part = turned[q * slab : (q + 1) * slab]
                if m == 0:
                    part = (1.0 - part * (2.0 / (BANDS * (REPEATS - 1)))) * masks[q]
                    flow[...] += jnp.sum(part.reshape(slab // 8, 8, TILE), axis=0)
                elif m == 1:
                    part = part * (masks[q] * (1.0 / (BANDS * REPEATS * math.sqrt(BAND_BINS))))
                else:
                    part = part * (masks[q] * (0.5 / (REPEATS * BANDS * VARIANCE_SCALE * BAND_BINS)))
                outbox[q * RING + group, s, m] = part

        @pl.when(step == 0)
        def _():
            pl.semaphore_wait(barrier, n_ascan + n_scan - 2)

        @pl.when(step < RING * scans - HELD)
        def _():
            send(group, s)

    rows = jnp.sum((bottom_ref[...] - top_ref[...]).astype(jnp.float32), axis=0, keepdims=True)
    own_stat[pl.ds(0, 1), :] = jnp.sum(flow[...], axis=0, keepdims=True)
    own_stat[pl.ds(1, 1), :] = rows * float(TILE)
    stat_a[my_scan] = own_stat[...]

    def a_copy(source, to, k):
        return pltpu.make_async_remote_copy(
            src_ref=own_stat, dst_ref=stat_a.at[source],
            send_sem=send_a.at[k], recv_sem=recv_a.at[source],
            device_id=(to, me), device_id_type=MESH,
        )

    def b_copy(source, to, k):
        return pltpu.make_async_remote_copy(
            src_ref=line_stat, dst_ref=stat_b.at[source],
            send_sem=send_b.at[k], recv_sem=recv_b.at[source],
            device_id=(my_scan, to), device_id_type=MESH,
        )

    @pl.loop(1, n_scan)
    def _(d):
        a_copy(my_scan, lax.rem(my_scan + d, n_scan), d).start()

    @pl.loop(1, n_scan)
    def _(d):
        a_copy(lax.rem(my_scan + d, n_scan), lax.rem(my_scan + d, n_scan), d).wait_recv()

    line_stat[...] = jnp.sum(stat_a[...], axis=0)
    stat_b[me] = line_stat[...]

    @pl.loop(1, n_ascan)
    def _(d):
        b_copy(me, lax.rem(me + d, n_ascan), d).start()

    @pl.loop(RING * scans - HELD, RING * scans)
    def _(step):
        send(group_of(step), scan_of(step))

    @pl.loop(1, n_scan)
    def _(d):
        a_copy(my_scan, lax.rem(my_scan + d, n_scan), d).wait_send()

    @pl.loop(1, n_ascan)
    def _(d):
        other = lax.rem(me + d, n_ascan)
        b_copy(other, other, d).wait_recv()

    stat_ref[...] = jnp.sum(stat_b[...], axis=0)

    @pl.loop(1, n_ascan)
    def _(d):
        other = lax.rem(me + d, n_ascan)
        b_copy(me, other, d).wait_send()
        for s in range(scans):
            block_copy(s, me, other).wait_send()

    @pl.loop(1, n_ascan)
    def _(d):
        other = lax.rem(me + d, n_ascan)
        for s in range(scans):
            block_copy(s, other, other).wait_recv()


def finish_kernel(maps_ref, stat_ref, angiogram_ref, structure_ref, speckle_ref, mean_ref, smooth, plain_sem, smooth_sem):
    scans, slab, width = angiogram_ref.shape
    block = smooth.shape[2]
    copies = [
        pltpu.make_async_copy(maps_ref.at[1], structure_ref, plain_sem.at[0]),
        pltpu.make_async_copy(maps_ref.at[2], speckle_ref, plain_sem.at[1]),
    ]
    for c in copies:
        c.start()
    totals = jnp.sum(stat_ref[...], axis=1, keepdims=True)
    mean = totals[0:1] / totals[1:2]
    scale = 1.0 / (3.0 * mean)
    mean_ref[...] = mean
    lane = lax.broadcasted_iota(jnp.int32, (8, width), 1)
    for s in range(scans):
        for k in range(slab // block):
            for z in range(0, block, 8):
                x = maps_ref[0, s, pl.ds(k * block + z, 8), :]
                before = jnp.where(lane == 0, 0.0, pltpu.roll(x, 1, 1))
                after = jnp.where(lane == width - 1, 0.0, pltpu.roll(x, width - 1, 1))
                smooth[s, k, pl.ds(z, 8), :] = (before + x + after) * scale
            c = pltpu.make_async_copy(
                smooth.at[s, k], angiogram_ref.at[s, pl.ds(k * block, block)], smooth_sem.at[s, k]
            )
            c.start()
            copies.append(c)
    for c in copies:
        c.wait()


def solution(mesh):
    n_scan, n_ascan = mesh.shape["scan"], mesh.shape["ascan"]

    def body(spectra, top, bottom):
        scans, repeats, lines, bins = spectra.shape
        slab = DEPTH // n_ascan
        width = lines * n_ascan
        f32 = jnp.float32
        vmem = pl.BlockSpec(memory_space=pltpu.VMEM)
        hbm = pl.BlockSpec(memory_space=pltpu.HBM)
        maps, stat = pl.pallas_call(
            functools.partial(exchange_kernel, n_scan, n_ascan, scans, slab),
            out_shape=(
                jax.ShapeDtypeStruct((3, scans, slab, width), f32),
                jax.ShapeDtypeStruct((2, TILE), f32),
            ),
            in_specs=[hbm] * 4,
            out_specs=(vmem, vmem),
            scratch_shapes=[
                pltpu.VMEM((scans, BANDS, REPEATS, TILE, BAND_BINS), jnp.bfloat16),
                pltpu.VMEM((RING, BAND_BINS, 2 * TILE), jnp.bfloat16),
                pltpu.VMEM((scans, TILE), jnp.int32),
                pltpu.VMEM((scans, TILE), jnp.int32),
                pltpu.VMEM((BANDS, REPEATS * TILE, 2 * TILE), f32),
                pltpu.VMEM((3, TILE, TILE), f32),
                pltpu.VMEM((n_ascan, scans, 3, slab, TILE), f32),
                pltpu.VMEM((8, TILE), f32),
                pltpu.VMEM((2, TILE), f32),
                pltpu.VMEM((2, TILE), f32),
                pltpu.VMEM((n_scan, 2, TILE), f32),
                pltpu.VMEM((n_ascan, 2, TILE), f32),
                pltpu.SemaphoreType.DMA((scans, BANDS)),
                pltpu.SemaphoreType.DMA((RING,)),
                pltpu.SemaphoreType.DMA((2,)),
                pltpu.SemaphoreType.DMA((n_ascan, scans)),
                pltpu.SemaphoreType.DMA((n_ascan, scans)),
                pltpu.SemaphoreType.DMA((n_scan,)),
                pltpu.SemaphoreType.DMA((n_scan,)),
                pltpu.SemaphoreType.DMA((n_ascan,)),
                pltpu.SemaphoreType.DMA((n_ascan,)),
            ],
            compiler_params=pltpu.CompilerParams(
                collective_id=0, has_side_effects=True, vmem_limit_bytes=40 * 2**20
            ),
            name="exchange",
        )(*(pltpu.with_memory_space_constraint(a, pltpu.HBM) for a in (spectra, make_table(), top, bottom)))

        angiogram, structure, speckle, mean = pl.pallas_call(
            finish_kernel,
            out_shape=[jax.ShapeDtypeStruct((scans, slab, width), f32)] * 3
            + [jax.ShapeDtypeStruct((1, 1), f32)],
            in_specs=[vmem, vmem],
            out_specs=[hbm] * 3 + [vmem],
            scratch_shapes=[
                pltpu.VMEM((scans, slab // 16, 16, width), f32),
                pltpu.SemaphoreType.DMA((2,)),
                pltpu.SemaphoreType.DMA((scans, slab // 16)),
            ],
            compiler_params=pltpu.CompilerParams(vmem_limit_bytes=8 * 2**20),
            name="finish",
        )(maps, stat)
        return angiogram, structure, speckle, mean.reshape(())

    return jax.shard_map(
        body,
        mesh=mesh,
        in_specs=(P("scan", None, "ascan", None), P("scan", "ascan"), P("scan", "ascan")),
        out_specs=(P("scan", "ascan", None),) * 3 + (P(),),
        check_vma=False,
    )
```

time: 91.2 us -> 88.4 us (0.969)
  Pallas kernels: 89.6 us -> 87.7 us
    pallas_call x1, Pallas kernels: 4.45 us -> 2.53 us  [body(): pl.pallas_call(finish_kernel, out_shape=[jax.ShapeDtypeStruct((scans, sla...]
where the time goes in v3:
time: 88.4 us; the launch traced here: 88.3 us
  Pallas kernels  87.7 us (99%)
    pallas_call x1, Pallas kernels, body(): pl.pallas_call(functools.partial(exchange_kernel, n_scan, n_ascan, scans,...  85.1 us
    pallas_call x1, Pallas kernels, body(): pl.pallas_call(finish_kernel, out_shape=[jax.ShapeDtypeStruct((scans, sla...  2.53 us

profile of v3, /device:TPU:32, one launch (start us, length us, event | category | flops | bytes accessed | tf_op | source)
XLA Modules:
  0.0 88.3 jit_solution(14249376330492482373)
XLA Ops:
  0.6 85.1 %exchange.1 = (f32[3,2,32,4096]{3,2,1,0:T(8,128)S(1)}, f32[2,128]{1,0:T(2,128)S(1)}) custom-call(bf16[2,4,128,2048]{3,2,1,0:T(8,128)(2,1)} %spectra_hbm.1, bf16[8,512,256]{2,1,0:T(8,128)(2,1)} %constant.2.clone.table_hbm, s32[2,128]{1,0:T(2,128)} %top_hbm.1, s32[2,128]{1,0:T(2,128)} %bottom_hbm.1), custom_call_target="tpu_custom_call" | custom-call | tf_op jit(solution)/shard_map/exchange/pallas_call | solution.py:307
  85.8 2.5 %finish.1 = (f32[2,32,4096]{2,1,0:T(8,128)}, f32[2,32,4096]{2,1,0:T(8,128)}, f32[2,32,4096]{2,1,0:T(8,128)}, f32[1,1]{1,0:T(1,128)}) custom-call(f32[3,2,32,4096]{3,2,1,0:T(8,128)S(1)} %get-tuple-element.10.maps_ref, f32[2,128]{1,0:T(2,128)S(1)} %get-tuple-element.11.stat_ref), custom_call_target="tpu_custom_call" | custom-call | tf_op jit(solution)/shard_map/finish/pallas_call | solution.py:344

commit v4 on v3

--- a/solution.py
+++ b/solution.py
@@ -60,17 +60,6 @@
     def scan_of(step):
         return jnp.where(step < 6 * scans, lax.rem(step // 2, scans), lax.rem(step, scans))
 
-
-    barrier = pltpu.get_barrier_semaphore()
-
-    @pl.loop(1, n_ascan)
-    def _(d):
-        pl.semaphore_signal(barrier, inc=1, device_id=(my_scan, lax.rem(me + d, n_ascan)), device_id_type=MESH)
-
-    @pl.loop(1, n_scan)
-    def _(d):
-        pl.semaphore_signal(barrier, inc=1, device_id=(lax.rem(my_scan + d, n_scan), me), device_id_type=MESH)
-
     def table_copy(tile):
         return pltpu.make_async_copy(table_hbm.at[tile], table.at[tile], table_sem.at[tile])
 
@@ -85,12 +74,23 @@
         pltpu.make_async_copy(bottom_hbm, bottom_ref, surface_sem.at[1]),
     )
     table_copy(group_of(0)).start()
-    for s in range(scans):
+    for band in range(BANDS):
+        spectra_copy(0, band).start()
+
+    barrier = pltpu.get_barrier_semaphore()
+    for along in (4, 5, 3, 6, 2, 7, 1, 0):
+        for across in (2, 1, 3, 0):
+            if along or across:
+                to = lax.rem(row + across, per_tile) * RING + lax.rem(place + along, RING)
+                pl.semaphore_signal(barrier, inc=1, device_id=(my_scan, to), device_id_type=MESH)
+    for d in range(1, n_scan):
+        pl.semaphore_signal(barrier, inc=1, device_id=(lax.rem(my_scan + d, n_scan), me), device_id_type=MESH)
+
+    for c in surface_copies:
+        c.start()
+    for s in range(1, scans):
         for band in range(BANDS):
             spectra_copy(s, band).start()
-        if s == 0:
-            for c in surface_copies:
-                c.start()
 
     @pl.loop(1, RING)
     def _(d):
@@ -193,11 +193,15 @@
                     part = part * (masks[q] * (0.5 / (REPEATS * BANDS * VARIANCE_SCALE * BAND_BINS)))
                 outbox[q * RING + group, s, m] = part
 
-        @pl.when(step == 0)
+        @pl.when(step == 1)
         def _():
             pl.semaphore_wait(barrier, n_ascan + n_scan - 2)
 
-        @pl.when(step < RING * scans - HELD)
+            @pl.loop(0, 1)
+            def _(early):
+                send(group_of(early), scan_of(early))
+
+        @pl.when((step >= 1) & (step < RING * scans - HELD))
         def _():
             send(group, s)
 
@@ -248,7 +252,10 @@
         other = lax.rem(me + d, n_ascan)
         b_copy(other, other, d).wait_recv()
 
-    stat_ref[...] = jnp.sum(stat_b[...], axis=0)
+    totals = jnp.sum(jnp.sum(stat_b[...], axis=0), axis=1, keepdims=True)
+    mean = totals[0:1] / totals[1:2]
+    stat_ref[pl.ds(0, 1), :] = jnp.broadcast_to(mean, (1, TILE))
+    stat_ref[pl.ds(1, 1), :] = jnp.broadcast_to(1.0 / (3.0 * mean), (1, TILE))
 
     @pl.loop(1, n_ascan)
     def _(d):
@@ -273,10 +280,8 @@
     ]
     for c in copies:
         c.start()
-    totals = jnp.sum(stat_ref[...], axis=1, keepdims=True)
-    mean = totals[0:1] / totals[1:2]
-    scale = 1.0 / (3.0 * mean)
-    mean_ref[...] = mean
+    mean_ref[...] = stat_ref[pl.ds(0, 1), pl.ds(0, 1)]
+    scale = jnp.tile(jnp.broadcast_to(stat_ref[pl.ds(1, 1), :], (8, TILE)), (1, maps_ref.shape[3] // TILE))
     lane = lax.broadcasted_iota(jnp.int32, (8, width), 1)
     for s in range(scans):
         for k in range(slab // block):

time: 88.4 us -> 86.4 us (0.977)
  Pallas kernels: 87.7 us -> 85.7 us
    pallas_call x1, Pallas kernels: 85.1 us -> 83.1 us  [body(): pl.pallas_call(functools.partial(exchange_kernel, n_scan, n_ascan, scans,...]
where the time goes in v4:
time: 86.4 us; the launch traced here: 86.3 us
  Pallas kernels  85.7 us (99%)
    pallas_call x1, Pallas kernels, body(): pl.pallas_call(functools.partial(exchange_kernel, n_scan, n_ascan, scans,...  83.1 us
    pallas_call x1, Pallas kernels, body(): pl.pallas_call(finish_kernel, out_shape=[jax.ShapeDtypeStruct((scans, sla...  2.51 us

profile of v4, /device:TPU:32, one launch (start us, length us, event | category | flops | bytes accessed | tf_op | source)
XLA Modules:
  0.0 86.3 jit_solution(1009592833570705447)
XLA Ops:
  0.6 83.1 %exchange.1 = (f32[3,2,32,4096]{3,2,1,0:T(8,128)S(1)}, f32[2,128]{1,0:T(2,128)S(1)}) custom-call(bf16[2,4,128,2048]{3,2,1,0:T(8,128)(2,1)} %spectra_hbm.1, bf16[8,512,256]{2,1,0:T(8,128)(2,1)} %constant.2.clone.table_hbm, s32[2,128]{1,0:T(2,128)} %top_hbm.1, s32[2,128]{1,0:T(2,128)} %bottom_hbm.1), custom_call_target="tpu_custom_call" | custom-call | tf_op jit(solution)/shard_map/exchange/pallas_call | solution.py:312
  83.8 2.5 %finish.1 = (f32[2,32,4096]{2,1,0:T(8,128)}, f32[2,32,4096]{2,1,0:T(8,128)}, f32[2,32,4096]{2,1,0:T(8,128)}, f32[1,1]{1,0:T(1,128)}) custom-call(f32[3,2,32,4096]{3,2,1,0:T(8,128)S(1)} %get-tuple-element.10.maps_ref, f32[2,128]{1,0:T(2,128)S(1)} %get-tuple-element.11.stat_ref), custom_call_target="tpu_custom_call" | custom-call | tf_op jit(solution)/shard_map/finish/pallas_call | solution.py:349
